TPU v7x, 8 devices: a whole 2x2x1 slice. The times are simulated.
8 devices in a mesh: dp: 1 (over z), ep: 8 (over y, x, core).
Axes of the slice: x: 2, y: 2, z: 1, core: 2. Of those that a mesh axis runs over, the one named last changes fastest.
Arguments:
- x_in: bfloat16 [1024, 2048], P(('dp', 'ep'))
- expert_ids: int32 [1024, 6], P(('dp', 'ep'))
- norm_weight: bfloat16 [2048], replicated
- router_w: bfloat16 [2048, 64], replicated
- router_b: bfloat16 [64], replicated
- w_gate_up: bfloat16 [64, 2048, 2816], P('ep')
- b_gate_up: bfloat16 [64, 2816], P('ep')
- w_down: bfloat16 [64, 1408, 2048], P('ep')
- b_down: bfloat16 [64, 2048], P('ep')
Outputs:
- output: bfloat16 [1024, 2048], P(('dp', 'ep'))
All inputs are finite; a program needn't handle non-finite values.
Results may differ from a plain program's by a relative error of at most 0.00655539.
Values are sent between devices in bfloat16 or wider.
A program may use at most 1 GiB of HBM per device.

v0:
```python
import jax
import jax.numpy as jnp
from jax import lax
from jax.sharding import PartitionSpec as P

CAPACITY_FACTOR = 4
EPSILON = 1e-5
LIMIT = 7.0
ALPHA = 1.702


def rms_norm(x_in, norm_weight):
    x_float = x_in.astype(jnp.float32)
    inv_rms = lax.rsqrt(jnp.mean(x_float * x_float, axis=-1, keepdims=True) + EPSILON)
    return (x_float * inv_rms * norm_weight.astype(jnp.float32)).astype(jnp.bfloat16)


def route_gates(hidden, expert_ids, router_w, router_b):
    logits = jnp.dot(hidden, router_w, preferred_element_type=jnp.float32) + router_b.astype(jnp.float32)
    return jax.nn.softmax(jnp.take_along_axis(logits, expert_ids, axis=1), axis=-1)


def clamped_glu(gate_up):
    gate = jnp.minimum(gate_up[..., 0::2].astype(jnp.float32), LIMIT)
    linear = jnp.clip(gate_up[..., 1::2].astype(jnp.float32), -LIMIT, LIMIT)
    return (gate * jax.nn.sigmoid(ALPHA * gate) * (linear + 1.0)).astype(jnp.bfloat16)


def slot_tables(flat_ids, experts, capacity):
    pairs = flat_ids.shape[0]
    onehot = (flat_ids[:, None] == jnp.arange(experts, dtype=jnp.int32)[None, :]).astype(jnp.int32)
    rank = jnp.sum((jnp.cumsum(onehot, axis=0) - 1) * onehot, axis=1)
    slot_pair = jnp.zeros((experts * capacity,), jnp.int32).at[flat_ids * capacity + rank].set(jnp.arange(pairs, dtype=jnp.int32))
    return slot_pair, rank, jnp.sum(onehot, axis=0)


def mix_residual(x_in, gates, picked):
    mixed = jnp.sum(gates[:, :, None] * picked.astype(jnp.float32), axis=1)
    return (x_in.astype(jnp.float32) + mixed).astype(jnp.bfloat16)


def solution(mesh):
    n_group = mesh.shape['ep']
    rows_spec = P(('dp', 'ep'), None)

    def local_block(x_in, expert_ids, norm_weight, router_w, router_b, w_gate_up, b_gate_up, w_down, b_down):
        tok_dev, d_model = x_in.shape
        top_k = expert_ids.shape[1]
        local_exp = w_gate_up.shape[0]
        experts = local_exp * n_group
        capacity = CAPACITY_FACTOR * top_k * tok_dev // experts
        hidden = rms_norm(x_in, norm_weight)
        gates = route_gates(hidden, expert_ids, router_w, router_b)
        flat_ids = expert_ids.reshape(-1)
        slot_pair, rank, _ = slot_tables(flat_ids, experts, capacity)
        rows = jnp.take(hidden, slot_pair // top_k, axis=0).reshape(n_group, local_exp, capacity, d_model)
        received = lax.all_to_all(rows, 'ep', 0, 0, tiled=True)
        gate_up = (jnp.einsum('sgcd,gdf->gscf', received, w_gate_up, preferred_element_type=jnp.float32) + b_gate_up[:, None, None, :].astype(jnp.float32)).astype(jnp.bfloat16)
        expert_out = (jnp.einsum('gscf,gfd->gscd', clamped_glu(gate_up), w_down, preferred_element_type=jnp.float32) + b_down[:, None, None, :].astype(jnp.float32)).astype(jnp.bfloat16)
        returned = lax.all_to_all(expert_out, 'ep', 1, 1, tiled=True)
        back_slot = ((flat_ids % local_exp) * n_group + flat_ids // local_exp) * capacity + rank
        picked = jnp.take(returned.reshape(-1, d_model), back_slot, axis=0).reshape(tok_dev, top_k, d_model)
        return mix_residual(x_in, gates, picked)

    return jax.shard_map(local_block, mesh=mesh, in_specs=(rows_spec, rows_spec, P(), P(), P(), P('ep', None, None), P('ep', None), P('ep', None, None), P('ep', None)), out_specs=rows_spec, check_vma=False)
```

profile of v0, /device:TPU:0, one launch (start us, length us, event | category | flops | bytes accessed | tf_op | source)
XLA Modules:
  0.0 1084.6 jit_solution(8415199369585716160)
XLA Ops:
  0.0 0.0 copy-start
  0.0 0.8 copy.42
  0.8 0.1 reshape.245
  1.0 0.1 eq.28
  1.1 0.1 reshape.243
  1.3 1.8 reduce-window.6
  3.1 0.3 slice_reduce_fusion
  3.4 0.1 fusion.18
  3.5 0.0 copy-start.6
  3.5 0.6 fusion.34
  4.2 0.0 copy-done.6
  4.2 3.4 scatter_custom_fusion
  7.6 1.2 fusion.13
  8.9 0.7 convert_element_type.48
  9.6 0.1 broadcast_in_dim.44
  9.7 1.2 fusion.15
  10.9 0.0 copy-start.1
  10.9 16.0 %gather_fusion = bf16[3072,2048]{1,0:T(8,128)(2,1)} fusion(bf16[128,2048]{1,0:T(8,128)(2,1)S(1)} %fusion.15, s32[3072]{0:T(1024)S(1)} %broadcast_clamp_fusion), kind=kCustom, calls=%fused_computation | custom fusion | bytes 25178112 | tf_op jit(solution)/shard_map/jit(_take)/gather | solution.py:56
  26.9 0.0 copy-done.1
  26.9 10.8 broadcast_select_fusion
  37.6 0.0 copy-start.8
  37.6 0.0 copy-start.5
  37.6 4.4 all-to-all-start
  42.1 0.0 copy-done.8
  42.1 0.6 convert_element_type.57
  42.7 0.0 copy-done.5
  42.7 139.4 %all-to-all-done = bf16[8,8,48,2048]{3,2,1,0:T(8,128)(2,1)} async-done(((bf16[8,8,48,2048]{3,2,1,0:T(8,128)(2,1)}), bf16[8,8,48,2048]{3,2,1,0:T(8,128)(2,1)}, u32[]{:S(2)}, u32[]{:S(2)}) %all-to-all-start) | async-done | bytes 12582944 | tf_op jit(solution)/shard_map/all_to_all | solution.py:57
  182.1 50.0 %add_convert_fusion = bf16[8,8,48,2816]{3,2,1,0:T(8,128)(2,1)} fusion(f32[8,2816]{1,0:T(8,128)S(1)} %convert_element_type.52, bf16[8,2048,2816]{2,1,0:T(8,128)(2,1)} %param.14, bf16[8,8,48,2048]{3,2,1,0:T(8,128)(2,1)} %all-to-all-done), kind=kOutput, calls=%fused_computation.8 | convolution fusion | flops 35450781696 | bytes 122249216 | tf_op jit(solution)/shard_map/sgcd,gdf->gscf/dot_general | solution.py:58
  232.1 313.7 %slice.15 = bf16[8,8,48,1408]{3,2,1,0:T(8,128)(2,1)} slice(bf16[8,8,48,2816]{3,2,1,0:T(8,128)(2,1)} %add_convert_fusion), slice={[0:8:1], [0:8:1], [0:48:1], [1:2816:2]} | slice | bytes 17301504 | tf_op jit(solution)/shard_map/slice | solution.py:25
  545.9 0.0 copy-start.4
  545.9 313.9 %slice.14 = bf16[8,8,48,1408]{3,2,1,0:T(8,128)(2,1)} slice(bf16[8,8,48,2816]{3,2,1,0:T(8,128)(2,1)} %add_convert_fusion), slice={[0:8:1], [0:8:1], [0:48:1], [0:2816:2]} | slice | bytes 17301504 | tf_op jit(solution)/shard_map/slice | solution.py:24
  859.8 0.0 copy-done.4
  859.8 36.6 %add_convert_fusion.1 = bf16[8,8,48,2048]{3,2,1,0:T(8,128)(2,1)} fusion(f32[8,2048]{1,0:T(8,128)S(1)} %copy-done.4, bf16[8,1408,2048]{2,1,0:T(8,128)(2,1)} %param.16, bf16[8,8,48,1408]{3,2,1,0:T(8,128)(2,1)} %slice.15, bf16[8,8,48,1408]{3,2,1,0:T(8,128)(2,1)} %slice.14), kind=kOutput, calls=%fused_computation.9 | convolution fusion | flops 17781227520 | bytes 76087296 | tf_op jit(solution)/shard_map/gscf,gfd->gscd/dot_general | solution.py:59
  896.4 10.8 copy.49
  907.2 0.0 copy-start.7
  907.2 0.0 copy-start.10
  907.2 0.0 copy-start.3
  907.2 0.0 copy-start.2
  907.2 4.5 all-to-all-start.1
  911.7 0.0 copy-done.7
  911.7 0.1 reduce_sum.43
  911.8 0.0 copy-done.10
  911.8 0.0 copy-done.3
  911.9 0.1 copy.39
  912.0 0.1 reshape.263
  912.1 0.1 copy.45
  912.2 0.1 copy.46
  912.4 0.0 copy-done
  912.4 0.0 copy-done.2
  912.4 0.3 convolution_add_fusion
  912.7 0.0 copy-start.9
  912.7 5.1 gather_fusion.2
  917.8 0.1 reshape.266
  918.0 0.1 copy.40
  918.1 0.1 copy.41
  918.2 0.0 copy-done.9
  918.2 132.1 %all-to-all-done.1 = bf16[8,8,48,2048]{3,2,0,1:T(8,128)(2,1)} async-done(((bf16[8,8,48,2048]{3,2,0,1:T(8,128)(2,1)}), bf16[8,8,48,2048]{3,2,0,1:T(8,128)(2,1)}, u32[]{:S(2)}, u32[]{:S(2)}) %all-to-all-start.1) | async-done | bytes 12582944 | tf_op jit(solution)/shard_map/all_to_all | solution.py:60
  1050.4 10.8 copy.50
  1061.2 12.5 %gather_fusion.1 = bf16[768,2048]{1,0:T(8,128)(2,1)S(1)} fusion(bf16[3072,2048]{1,0:T(8,128)(2,1)} %bitcast.39, s32[1024]{0:T(1024)S(1)} %pad_clamp_fusion), kind=kCustom, calls=%fused_computation.1 | custom fusion | bytes 6294528 | tf_op jit(solution)/shard_map/jit(_take)/gather | solution.py:62
  1073.7 2.9 gather.20
  1076.6 6.0 multiply_reduce_fusion
  1082.6 2.0 fusion.16
  (14 shorter events, 0.2 us)
Async XLA Ops:
  0.0 912.4 %copy-start = (bf16[2048,64]{0,1:T(8,128)(2,1)S(1)}, bf16[2048,64]{0,1:T(8,128)(2,1)}, u32[]{:S(2)}) copy-start(bf16[2048,64]{0,1:T(8,128)(2,1)} %param.12) | copy-start | bytes 786436
  3.5 0.6 copy-start.6
  10.9 16.0 %copy-start.1 = (bf16[128,2048]{1,0:T(8,128)(2,1)}, bf16[128,2048]{1,0:T(8,128)(2,1)S(1)}, u32[]{:S(2)}) copy-start(bf16[128,2048]{1,0:T(8,128)(2,1)S(1)} %fusion.15) | copy-start | bytes 1572868
  37.6 4.4 copy-start.8
  37.6 5.1 copy-start.5
  37.6 144.5 %all-to-all-start = ((bf16[8,8,48,2048]{3,2,1,0:T(8,128)(2,1)}), bf16[8,8,48,2048]{3,2,1,0:T(8,128)(2,1)}, u32[]{:S(2)}, u32[]{:S(2)}) async-start(bf16[8,8,48,2048]{3,2,1,0:T(8,128)(2,1)} %broadcast_select_fusion), calls=%async_computation | async-start | bytes 25165824 | tf_op jit(solution)/shard_map/all_to_all | solution.py:57
  545.9 313.9 %copy-start.4 = (f32[8,2048]{1,0:T(8,128)S(1)}, f32[8,2048]{1,0:T(8,128)}, u32[]{:S(2)}) copy-start(f32[8,2048]{1,0:T(8,128)} %convert_element_type.57) | copy-start | bytes 196612
  907.2 4.5 copy-start.7
  907.2 4.7 copy-start.10
  907.2 4.7 copy-start.3
  907.2 5.2 copy-start.2
  907.2 143.2 %all-to-all-start.1 = ((bf16[8,8,48,2048]{3,2,0,1:T(8,128)(2,1)}), bf16[8,8,48,2048]{3,2,0,1:T(8,128)(2,1)}, u32[]{:S(2)}, u32[]{:S(2)}) async-start(bf16[8,8,48,2048]{3,2,0,1:T(8,128)(2,1)} %copy.49), calls=%async_computation.1 | async-start | bytes 25165824 | tf_op jit(solution)/shard_map/all_to_all | solution.py:60
  912.7 5.5 copy-start.9
where the time goes:
time: 1090 us; the launch traced here: 1080 us
  local copies, waits for them, and re-layouts  692 us (63%)
  waiting for transfers between devices  272 us (25%)
  matrix products  86.9 us (8%)
  other arithmetic  25.3 us (2%)
    slice x1, local copies, waits for them, and re-layouts, clamped_glu(): gate = jnp.minimum(gate_up[..., 0::2].astype(jnp.float32), LIMIT)  314 us
    slice x1, local copies, waits for them, and re-layouts, clamped_glu(): linear = jnp.clip(gate_up[..., 1::2].astype(jnp.float32), -LIMIT, LIMIT)  314 us
    all_to_all x1, waiting for transfers between devices, local_block(): received = lax.all_to_all(rows, 'ep', 0, 0, tiled=True)  139 us
    all_to_all x1, waiting for transfers between devices, local_block(): returned = lax.all_to_all(expert_out, 'ep', 1, 1, tiled=True)  132 us
    dot_general x1, matrix products, local_block(): jnp.einsum('sgcd,gdf->gscf', received, w_gate_up, preferred_element_type=...  50 us
    dot_general x1, matrix products, local_block(): jnp.einsum('gscf,gfd->gscd', clamped_glu(gate_up), w_down, preferred_elem...  36.6 us
  transfers between devices with their start and end apart: 2, of which 2 were waited for; matrix products, arithmetic and copies ran while one was open for 1% of the time, Pallas kernels for 0%

commit v1 on v0

v1 whole, which is shorter than its diff:
```python
import functools

import jax
import jax.numpy as jnp
from jax import lax
from jax.experimental import pallas as pl
from jax.experimental.pallas import tpu as pltpu
from jax.sharding import PartitionSpec as P

CAPACITY_FACTOR = 4
EPSILON = 1e-5
LIMIT = 7.0
ALPHA = 1.702
LOWEST = -3.3895313892515355e38
BLK = 16
CHUNK = 128
COLS = 256
MESH = pl.DeviceIdType.MESH
F32 = jnp.float32
BF16 = jnp.bfloat16
VMEM_LIMIT = 62 * 1024 * 1024


def flip(me, role):
    core = lax.rem(lax.rem(me, 2) + lax.rem(role, 2), 2)
    x = lax.rem(lax.rem(lax.div(me, 2), 2) + lax.rem(lax.div(role, 2), 2), 2)
    y = lax.rem(lax.div(me, 4) + lax.div(role, 4), 2)
    return y * 4 + x * 2 + core


def remote(src, dst, send, recv, device):
    return pltpu.make_async_remote_copy(src_ref=src, dst_ref=dst, send_sem=send, recv_sem=recv, device_id={'ep': device}, device_id_type=MESH)


def dispatch_kernel(top_k, local_exp, cap, x_hbm, ids_hbm, g_ref, wr_ref, br_ref, xs_hbm, pm_hbm, cnt_ref,
                    xb, idb, hb, wrp, brp, tri, oh, pt, probs, mask, stage, pstage,
                    lsem, osem, psem, ssem, rsem, isend, irecv):
    tok, d_model = x_hbm.shape
    experts = wr_ref.shape[1]
    half = tok // 2
    me = lax.axis_index('ep')
    load_x = pltpu.make_async_copy(x_hbm, xb.at[0], lsem.at[0])
    load_ids = pltpu.make_async_copy(ids_hbm, idb.at[0], lsem.at[1])
    load_x.start()
    load_ids.start()
    barrier = pltpu.get_barrier_semaphore()
    for r in range(1, 8):
        pl.semaphore_signal(barrier, inc=1, device_id={'ep': flip(me, r)}, device_id_type=MESH)
    load_x.wait()
    load_ids.wait()
    pl.semaphore_wait(barrier, 7)

    def piece(src_role, h, dst_role, to_role, k):
        rows = pl.ds(h * half, half)
        return remote(xb.at[src_role, rows], xb.at[dst_role, rows], ssem.at[k], rsem.at[dst_role, h], flip(me, to_role))

    def landed(role, h):
        piece(role, h, role, 1, 0).wait_recv()

    sends = [(0, 0, 2, 2), (0, 1, 4, 4), (0, 0, 1, 1), (0, 1, 1, 1), (0, 1, 2, 2), (0, 0, 4, 4)]
    relays = [(2, 0, 6, 4), (2, 0, 3, 1), (4, 1, 6, 2), (4, 1, 5, 1), (2, 1, 3, 1), (4, 0, 5, 1)]
    last = [(6, 0, 7, 1), (6, 1, 7, 1)]
    everything = sends + relays + last
    ids_out = [remote(idb.at[0], idb.at[r], isend.at[r], irecv.at[r], flip(me, r)) for r in range(1, 8)]
    for c in ids_out:
        c.start()

    def go(k):
        piece(*everything[k], k).start()

    for k in range(6):
        go(k)

    wrp[...] = jnp.zeros_like(wrp)
    wrp[:, :experts] = wr_ref[...]
    brp[...] = jnp.zeros_like(brp)
    brp[0:1, :experts] = br_ref[...].astype(F32)
    tri[...] = (lax.broadcasted_iota(jnp.int32, (tok, tok), 0) < lax.broadcasted_iota(jnp.int32, (tok, tok), 1)).astype(F32).astype(BF16)
    cnt_ref[...] = jnp.zeros_like(cnt_ref)

    def step(i, carry):
        @pl.when(i == 1)
        def _():
            landed(1, 0)
            landed(1, 1)

        @pl.when(i == 2)
        def _():
            landed(2, 0)
            go(6)
            go(7)
            landed(4, 1)
            go(8)
            go(9)
            landed(2, 1)
            go(10)
            landed(4, 0)
            go(11)

        @pl.when(i == 3)
        def _():
            landed(3, 0)
            landed(3, 1)

        @pl.when(i == 5)
        def _():
            landed(5, 0)
            landed(5, 1)

        @pl.when(i == 6)
        def _():
            landed(6, 0)
            go(12)
            landed(6, 1)
            go(13)

        @pl.when(i == 7)
        def _():
            landed(7, 0)
            landed(7, 1)

        @pl.when(i >= 1)
        def _():
            remote(idb.at[i], idb.at[i], isend.at[0], irecv.at[i], flip(me, 1)).wait_recv()

        src = flip(me, i)
        slot = lax.rem(i, 2)
        out_x = pltpu.make_async_copy(stage.at[slot], xs_hbm.at[:, src], osem.at[slot])
        out_p = pltpu.make_async_copy(pstage.at[slot], pm_hbm.at[src], psem.at[slot])

        def norm(j, c):
            rows = pl.ds(pl.multiple_of(j * BLK, BLK), BLK)
            xf = xb[i, rows, :].astype(F32)
            inv = lax.rsqrt(jnp.mean(xf * xf, axis=-1, keepdims=True) + EPSILON)
            hb[rows, :] = (xf * inv * g_ref[...].astype(F32)).astype(BF16)
            return c

        lax.fori_loop(0, tok // BLK, norm, 0)
        logits = jnp.dot(hb[...], wrp[...], preferred_element_type=F32) + brp[0:1, :]
        logits = jnp.transpose(logits)[:experts]
        ids = idb[i]
        expert_no = lax.broadcasted_iota(jnp.int32, (experts, tok), 0)
        chosen = jnp.zeros((experts, tok), F32)
        for k in range(top_k):
            chosen = jnp.where(expert_no == ids[k:k + 1, :], 1.0, chosen)
        picked = jnp.where(chosen > 0, logits, -jnp.inf)
        ex = jnp.exp(picked - jnp.max(picked, axis=0, keepdims=True))
        probs[...] = ex / jnp.sum(ex, axis=0, keepdims=True)
        mask[...] = chosen
        mine = pl.ds(pl.multiple_of(me * local_exp, local_exp), local_exp)
        p_loc = probs[mine, :]
        m_loc = mask[mine, :]
        rank = jnp.dot(m_loc.astype(BF16), tri[...], preferred_element_type=F32)
        count = jnp.sum(m_loc, axis=1, keepdims=True)
        lane = lax.broadcasted_iota(jnp.int32, cnt_ref.shape, 1)
        cnt_ref[...] = jnp.where(lane == src, count.astype(jnp.int32), cnt_ref[...])
        rank = jnp.where(m_loc > 0, rank, -1.0)
        number = lax.broadcasted_iota(jnp.int32, (cap, tok), 0).astype(F32)

        @pl.when(i >= 2)
        def _():
            out_x.wait()
            out_p.wait()

        for e in range(local_exp):
            hit = rank[e:e + 1, :] == number
            oh[e * cap:(e + 1) * cap, :] = jnp.where(hit, 1.0, 0.0).astype(BF16)
            pt[e * cap:(e + 1) * cap, :] = jnp.where(hit, p_loc[e:e + 1, :], 0.0)
        for b in range(local_exp * cap // tok):
            p = jnp.transpose(pt[b * tok:(b + 1) * tok, :])
            for part in range(3):
                low = p.astype(BF16)
                pstage[slot, part * tok:(part + 1) * tok, b * tok:(b + 1) * tok] = low
                p = p - low.astype(F32)
        for n in range(0, d_model, 512):
            rows = jnp.dot(oh[...], hb[:, n:n + 512], preferred_element_type=F32).astype(BF16)
            for e in range(local_exp):
                stage[slot, e, :, n:n + 512] = rows[e * cap:(e + 1) * cap, :]
        out_x.start()
        out_p.start()
        return carry

    lax.fori_loop(0, 8, step, 0)
    for slot in range(2):
        pltpu.make_async_copy(stage.at[slot], xs_hbm.at[:, me], osem.at[slot]).wait()
        pltpu.make_async_copy(pstage.at[slot], pm_hbm.at[me], psem.at[slot]).wait()
    for c in ids_out:
        c.wait_send()
    for k in range(len(everything)):
        piece(*everything[k], k).wait_send()


def gate_up_kernel(cnt_ref, xs_hbm, wgu_hbm, bgu_ref, z_hbm, wb, xbuf, xc, zc, zb, bias, perm, blk, wsem, xsem, zsem):
    local_exp, n_src, cap, d_model = xs_hbm.shape
    width = wgu_hbm.shape[2]
    rows_all = n_src * cap
    per_src = cap // BLK
    n_blk = rows_all // BLK
    n_slot = wb.shape[0]

    def load_w(e):
        slot = lax.rem(e, n_slot)
        return pltpu.make_async_copy(wgu_hbm.at[e], wb.at[slot], wsem.at[slot])

    def load_x(e):
        slot = lax.rem(e, 2)
        return pltpu.make_async_copy(xs_hbm.at[e], xbuf.at[slot], xsem.at[slot])

    def save_z(e):
        slot = lax.rem(e, 2)
        return pltpu.make_async_copy(zb.at[slot, pl.ds(0, rows_all)], z_hbm.at[e], zsem.at[slot])

    for e in range(2):
        load_x(e).start()
    for e in range(n_slot):
        load_w(e).start()
    bias[...] = bgu_ref[...].astype(F32)
    row = lax.broadcasted_iota(jnp.int32, perm.shape, 0)
    col = lax.broadcasted_iota(jnp.int32, perm.shape, 1)
    source = jnp.where(col < 128, 2 * col, 2 * col - 255)
    perm[...] = jnp.where(row == source, 1.0, 0.0).astype(BF16)

    def expert(e, carry):
        slot = lax.rem(e, n_slot)
        pair = lax.rem(e, 2)

        def listed(s, n):
            k = lax.div(cnt_ref[e, s] + (BLK - 1), BLK)
            for b in range(per_src):
                @pl.when(b < k)
                def _():
                    blk[n + b] = s * per_src + b
            return n + k

        total = lax.fori_loop(0, n_src, listed, 0)
        for j in range(CHUNK // BLK):
            blk[total + j] = n_blk

        @pl.when(e >= 2)
        def _():
            save_z(e - 2).wait()

        zb[pair] = jnp.zeros(zb.shape[1:], BF16)
        load_x(e).wait()
        load_w(e).wait()

        def chunk(c, carry):
            for j in range(CHUNK // BLK):
                b = jnp.minimum(blk[c * (CHUNK // BLK) + j], n_blk - 1)
                s = lax.div(b, per_src)
                first = pl.multiple_of(lax.rem(b, per_src) * BLK, BLK)
                xc[j * BLK:(j + 1) * BLK, :] = xbuf[pair, s, pl.ds(first, BLK), :]
            for n in range(0, width, 512):
                w = min(512, width - n)
                u = jnp.dot(xc[...], wb[slot, :, n:n + w], preferred_element_type=F32) + bias[pl.ds(e, 1), n:n + w]
                u = jnp.minimum(jnp.maximum(u, LOWEST), LIMIT).astype(BF16)
                for m in range(0, w, 256):
                    v = jnp.dot(u[:, m:m + 256], perm[...], preferred_element_type=F32)
                    gate = v[:, :128]
                    linear = jnp.maximum(v[:, 128:], -LIMIT)
                    z = gate * lax.logistic(ALPHA * gate) * (linear + 1.0)
                    zc[:, (n + m) // 2:(n + m) // 2 + 128] = z.astype(BF16)
            for j in range(CHUNK // BLK):
                b = blk[c * (CHUNK // BLK) + j]
                zb[pair, pl.ds(pl.multiple_of(b * BLK, BLK), BLK), :] = zc[j * BLK:(j + 1) * BLK, :]
            return carry

        lax.fori_loop(0, lax.div(total + (CHUNK // BLK - 1), CHUNK // BLK), chunk, 0)
        save_z(e).start()

        @pl.when(e + n_slot < local_exp)
        def _():
            load_w(e + n_slot).start()

        @pl.when(e + 2 < local_exp)
        def _():
            load_x(e + 2).start()
        return carry

    lax.fori_loop(0, local_exp, expert, 0)
    for e in range(local_exp - 2, local_exp):
        save_z(e).wait()


def combine_kernel(z_hbm, pm_hbm, wd_hbm, bd_ref, x_ref, out_ref,
                   zb, pm, wb, bias, yb, part, in0, in1, in2,
                   zsem, psem, wsem, s0, s1, s2, r0, r1, r2):
    local_exp, rows_all, d_ff = z_hbm.shape
    n_src = 8
    cap = rows_all // n_src
    tok, d_model = x_ref.shape
    n_col = d_model // COLS
    me = lax.axis_index('ep')
    barrier = pltpu.get_barrier_semaphore()
    for r in (1, 2, 4):
        pl.semaphore_signal(barrier, inc=1, device_id={'ep': flip(me, r)}, device_id_type=MESH)

    def load_w(c):
        slot = lax.rem(c, 2)
        cols = pl.ds(pl.multiple_of(c * COLS, COLS), COLS)
        return pltpu.make_async_copy(wd_hbm.at[:, :, cols], wb.at[slot], wsem.at[slot])

    load_w(0).start()
    zload = pltpu.make_async_copy(z_hbm, zb, zsem)
    pload = pltpu.make_async_copy(pm_hbm, pm, psem)
    zload.start()
    pload.start()
    bias[...] = bd_ref[...].astype(F32)

    def order(c):
        parity = lax.rem(c, 2)
        first = 2 + 2 * parity
        return first, 6 - first

    def to_mate(c):
        return remote(part.at[c, 1], in0.at[c], s0.at[c], r0.at[c], flip(me, 1))

    def to_first(c):
        return remote(part.at[c, 0, pl.ds(2, 2)], in1.at[c], s1.at[c], r1.at[c], flip(me, order(c)[0]))

    def to_second(c):
        return remote(part.at[c, 0, 1], in2.at[c], s2.at[c], r2.at[c], flip(me, order(c)[1]))

    def merge_mate(c):
        to_mate(c).wait_recv()
        for j in (2, 3, 0, 1):
            part[c, 0, j] = part[c, 0, j] + in0[c, j]
        to_first(c).start()

    def merge_first(c):
        to_first(c).wait_recv()
        for j in (1, 0):
            part[c, 0, j] = part[c, 0, j] + in1[c, j]
        to_second(c).start()

    def finish(c):
        to_second(c).wait_recv()
        cols = pl.ds(pl.multiple_of(c * COLS, COLS), COLS)
        out_ref[:, cols] = (x_ref[:, cols].astype(F32) + (part[c, 0, 0] + in2[c])).astype(BF16)

    def step(c, carry):
        slot = lax.rem(c, 2)
        cols = pl.ds(pl.multiple_of(c * COLS, COLS), COLS)

        @pl.when(c + 1 < n_col)
        def _():
            load_w(c + 1).start()

        @pl.when(c == 0)
        def _():
            zload.wait()
            pload.wait()

        load_w(c).wait()
        for e in range(local_exp):
            y = jnp.dot(zb[e], wb[slot, e], preferred_element_type=F32) + bias[e:e + 1, cols]
            y = y.astype(BF16)
            for s in range(n_src):
                yb[s, e * cap:(e + 1) * cap, :] = y[s * cap:(s + 1) * cap, :]
        first, second = order(c)
        for core in (1, 0):
            for j, base in enumerate((0, second, first, 6)):
                src = flip(me, base + core)
                sums = jnp.dot(pm[src], yb[src], preferred_element_type=F32)
                part[c, core, j] = (sums[2 * tok:] + sums[tok:2 * tok]) + sums[:tok]

        @pl.when(c == 0)
        def _():
            pl.semaphore_wait(barrier, 3)

        to_mate(c).start()

        @pl.when(c >= 1)
        def _():
            merge_mate(c - 1)

        @pl.when(c >= 3)
        def _():
            merge_first(c - 3)

        @pl.when(c >= 5)
        def _():
            finish(c - 5)
        return carry

    lax.fori_loop(0, n_col, step, 0)
    merge_mate(n_col - 1)
    for c in range(n_col - 3, n_col):
        merge_first(c)
    for c in range(n_col - 5, n_col):
        finish(c)
    for c in range(n_col):
        to_mate(c).wait_send()
        to_first(c).wait_send()
        to_second(c).wait_send()


def solution(mesh):
    n_group = mesh.shape['ep']
    assert n_group == 8
    rows_spec = P(('dp', 'ep'), None)

    def local_block(x_in, expert_ids, norm_weight, router_w, router_b, w_gate_up, b_gate_up, w_down, b_down):
        tok, d_model = x_in.shape
        top_k = expert_ids.shape[1]
        local_exp, _, width = w_gate_up.shape
        d_ff = w_down.shape[1]
        experts = local_exp * n_group
        cap = CAPACITY_FACTOR * top_k * tok // experts
        rows_all = n_group * cap
        ids_t = jnp.pad(expert_ids.T, ((0, 8 - top_k), (0, 0)), constant_values=-1)
        hbm = pl.BlockSpec(memory_space=pl.ANY)
        vmem = pl.BlockSpec(memory_space=pltpu.VMEM)
        smem = pl.BlockSpec(memory_space=pltpu.SMEM)
        dma = pltpu.SemaphoreType.DMA
        xs, pm, counts = pl.pallas_call(
            functools.partial(dispatch_kernel, top_k, local_exp, cap),
            out_shape=(jax.ShapeDtypeStruct((local_exp, n_group, cap, d_model), BF16),
                       jax.ShapeDtypeStruct((n_group, 3 * tok, local_exp * cap), BF16),
                       jax.ShapeDtypeStruct((local_exp, 128), jnp.int32)),
            in_specs=[hbm, hbm, vmem, vmem, vmem],
            out_specs=(hbm, hbm, vmem),
            scratch_shapes=[
                pltpu.VMEM((8, tok, d_model), BF16), pltpu.VMEM((8, 8, tok), jnp.int32), pltpu.VMEM((tok, d_model), BF16),
                pltpu.VMEM((d_model, 128), BF16), pltpu.VMEM((8, 128), F32), pltpu.VMEM((tok, tok), BF16),
                pltpu.VMEM((local_exp * cap, tok), BF16), pltpu.VMEM((local_exp * cap, tok), F32),
                pltpu.VMEM((experts, tok), F32), pltpu.VMEM((experts, tok), F32),
                pltpu.VMEM((2, local_exp, cap, d_model), BF16), pltpu.VMEM((2, 3 * tok, local_exp * cap), BF16),
                dma((2,)), dma((2,)), dma((2,)), dma((14,)), dma((8, 2)), dma((8,)), dma((8,))],
            compiler_params=pltpu.CompilerParams(collective_id=0, has_side_effects=True, vmem_limit_bytes=VMEM_LIMIT),
            name='dispatch',
        )(x_in, ids_t, norm_weight.reshape(1, d_model), router_w, router_b.reshape(1, experts))
        z = pl.pallas_call(
            gate_up_kernel,
            out_shape=jax.ShapeDtypeStruct((local_exp, rows_all, d_ff), BF16),
            in_specs=[smem, hbm, hbm, vmem],
            out_specs=hbm,
            scratch_shapes=[
                pltpu.VMEM((3, d_model, width), BF16), pltpu.VMEM((2, n_group, cap, d_model), BF16), pltpu.VMEM((CHUNK, d_model), BF16),
                pltpu.VMEM((CHUNK, d_ff), BF16), pltpu.VMEM((2, rows_all + BLK, d_ff), BF16), pltpu.VMEM((local_exp, width), F32),
                pltpu.VMEM((256, 256), BF16), pltpu.SMEM((rows_all // BLK + CHUNK // BLK,), jnp.int32),
                dma((3,)), dma((2,)), dma((2,))],
            compiler_params=pltpu.CompilerParams(vmem_limit_bytes=VMEM_LIMIT),
            name='gate_up',
        )(counts, xs, w_gate_up, b_gate_up)
        n_col = d_model // COLS
        return pl.pallas_call(
            combine_kernel,
            out_shape=jax.ShapeDtypeStruct((tok, d_model), BF16),
            in_specs=[hbm, hbm, hbm, vmem, vmem],
            out_specs=vmem,
            scratch_shapes=[
                pltpu.VMEM((local_exp, rows_all, d_ff), BF16), pltpu.VMEM((n_group, 3 * tok, local_exp * cap), BF16),
                pltpu.VMEM((2, local_exp, d_ff, COLS), BF16), pltpu.VMEM((local_exp, d_model), F32),
                pltpu.VMEM((n_group, local_exp * cap, COLS), BF16), pltpu.VMEM((n_col, 2, 4, tok, COLS), F32),
                pltpu.VMEM((n_col, 4, tok, COLS), F32), pltpu.VMEM((n_col, 2, tok, COLS), F32), pltpu.VMEM((n_col, tok, COLS), F32),
                dma, dma, dma((2,)), dma((n_col,)), dma((n_col,)), dma((n_col,)), dma((n_col,)), dma((n_col,)), dma((n_col,))],
            compiler_params=pltpu.CompilerParams(collective_id=1, has_side_effects=True, vmem_limit_bytes=VMEM_LIMIT),
            name='combine',
        )(z, pm, w_down, b_down, x_in)

    return jax.shard_map(local_block, mesh=mesh, in_specs=(rows_spec, rows_spec, P(), P(), P(), P('ep', None, None), P('ep', None), P('ep', None, None), P('ep', None)), out_specs=rows_spec, check_vma=False)
```

time: 1090 us -> 142 us (0.13)
  local copies, waits for them, and re-layouts: 692 us -> 6.4 us
  waiting for transfers between devices: 272 us -> 0 us
  Pallas kernels: 0 us -> 136 us
  matrix products: 86.9 us -> 0 us
  other arithmetic: 25.3 us -> 0 us
    slice x3 -> x0, local copies, waits for them, and re-layouts: 628 us -> none  [the longest x1 314 us: clamped_glu(): gate = jnp.minimum(gate_up[..., 0::2].astype(jnp.float32), LIMIT)]
    all_to_all x2 -> x0, waiting for transfers between devices: 272 us -> none  [the longest x1 139 us: local_block(): received = lax.all_to_all(rows, 'ep', 0, 0, tiled=True)]
    pallas_call x0 -> x3, Pallas kernels: none -> 136 us  [the longest x1 59.6 us: local_block(): pl.pallas_call(combine_kernel, out_shape=jax.ShapeDtypeStruct((tok, d_mod...]
    dot_general x3 -> x0, matrix products: 86.9 us -> none  [the longest x1 50 us: local_block(): jnp.einsum('sgcd,gdf->gscf', received, w_gate_up, preferred_element_type=...]
    gather x8 -> x0, local copies, waits for them, and re-layouts: 36.9 us -> none  [the longest x1 16 us: local_block(): jnp.take(hidden, slot_pair // top_k, axis=0)]
    select_n x2 -> x0, other arithmetic: 11.4 us -> none  [the longest x1 10.8 us: local_block(): jnp.take(hidden, slot_pair // top_k, axis=0)]
  transfers between devices with their start and end apart: 2 -> 0, of which waited for: 2 -> 0; matrix products, arithmetic and copies ran while one was open for 1% -> 0% of each run, Pallas kernels for 0% -> 0%
where the time goes in v1:
time: 142 us
  Pallas kernels  136 us (96%)
  local copies, waits for them, and re-layouts  6.4 us (5%)
    pallas_call x1, Pallas kernels, local_block(): pl.pallas_call(combine_kernel, out_shape=jax.ShapeDtypeStruct((tok, d_mod...  59.6 us
    pallas_call x1, Pallas kernels, local_block(): pl.pallas_call(gate_up_kernel, out_shape=jax.ShapeDtypeStruct((local_exp,...  43.3 us
    pallas_call x1, Pallas kernels, local_block(): pl.pallas_call(functools.partial(dispatch_kernel, top_k, local_exp, cap),...  32.7 us
    unnamed x2, local copies, waits for them, and re-layouts  3.83 us

profile of v1, /device:TPU:0, one launch (start us, length us, event | category | flops | bytes accessed | tf_op | source)
XLA Modules:
  0.0 142.1 jit_solution(13612112975179287485)
XLA Ops:
  0.0 1.3 pad.4.ids_hbm
  1.3 1.3 reshape.6.g_ref
  2.6 2.0 %copy.10.wr_ref = bf16[2048,64]{1,0:T(8,128)(2,1)} copy(bf16[2048,64]{0,1:T(8,128)(2,1)} %param.12) | data formatting | bytes 524288 | tf_op args[3]
  4.5 32.7 %dispatch.1 = (bf16[8,8,48,2048]{3,2,1,0:T(8,128)(2,1)}, bf16[8,384,384]{2,1,0:T(8,128)(2,1)}, s32[8,128]{1,0:T(8,128)}) custom-call(bf16[128,2048]{1,0:T(8,128)(2,1)} %x_ref.1, s32[8,128]{1,0:T(8,128)} %pad.4.ids_hbm, bf16[1,2048]{1,0:T(2,128)(2,1)} %reshape.6.g_ref, bf16[2048,64]{1,0:T(8,128)(2,1)} %copy.10.wr_ref, bf16[1,64]{1,0:T(2,128)(2,1)} %bitcast.3), custom_call_target="tpu_custom_call" | custom-call | tf_op jit(solution)/shard_map/dispatch/pallas_call | solution.py:416
  37.3 43.3 %gate_up.1.z_hbm = bf16[8,384,1408]{2,1,0:T(8,128)(2,1)} custom-call(s32[8,128]{1,0:T(8,128)} %get-tuple-element.8.cnt_ref, bf16[8,8,48,2048]{3,2,1,0:T(8,128)(2,1)} %get-tuple-element.9.xs_hbm, bf16[8,2048,2816]{2,1,0:T(8,128)(2,1)} %wgu_hbm.1, bf16[8,2816]{1,0:T(8,128)(2,1)} %bgu_ref.1), custom_call_target="tpu_custom_call" | custom-call | tf_op jit(solution)/shard_map/gate_up/pallas_call | solution.py:433
  80.6 59.6 %combine.1 = bf16[128,2048]{1,0:T(8,128)(2,1)} custom-call(bf16[8,384,1408]{2,1,0:T(8,128)(2,1)} %gate_up.1.z_hbm, bf16[8,384,384]{2,1,0:T(8,128)(2,1)} %get-tuple-element.10.pm_hbm, bf16[8,1408,2048]{2,1,0:T(8,128)(2,1)} %wd_hbm.1, bf16[8,2048]{1,0:T(8,128)(2,1)} %bd_ref.1, bf16[128,2048]{1,0:T(8,128)(2,1)} %x_ref.1), custom_call_target="tpu_custom_call" | custom-call | tf_op jit(solution)/shard_map/combine/pallas_call | solution.py:447
  140.3 1.9 %copy.12 = bf16[128,2048]{1,0:T(8,128)(2,1)} copy(bf16[128,2048]{1,0:T(8,128)(2,1)} %combine.1) | data formatting | bytes 1048576

commit v2 on v1

v2 whole, which is shorter than its diff:
```python
import functools

import jax
import jax.numpy as jnp
from jax import lax
from jax.experimental import pallas as pl
from jax.experimental.pallas import tpu as pltpu
from jax.sharding import PartitionSpec as P

CAPACITY_FACTOR = 4
EPSILON = 1e-5
LIMIT = 7.0
ALPHA = 1.702
LOWEST = -3.3895313892515355e38
BLK = 16
COLS = 256
MESH = pl.DeviceIdType.MESH
F32 = jnp.float32
BF16 = jnp.bfloat16
MIB = 1024 * 1024
N_RING = 3
NSTEP = 1024


def flip(me, role):
    core = lax.rem(lax.rem(me, 2) + lax.rem(role, 2), 2)
    x = lax.rem(lax.rem(lax.div(me, 2), 2) + lax.rem(lax.div(role, 2), 2), 2)
    y = lax.rem(lax.div(me, 4) + lax.div(role, 4), 2)
    return y * 4 + x * 2 + core


def remote(src, dst, send, recv, device):
    return pltpu.make_async_remote_copy(src_ref=src, dst_ref=dst, send_sem=send, recv_sem=recv, device_id={'ep': device}, device_id_type=MESH)


def dispatch_kernel(top_k, local_exp, cap, x_hbm, ids_hbm, g_hbm, wr_hbm, br_hbm, xs_ref, pm_hbm, cnt_hbm,
                    g_ref, wr_ref, br_ref, cnt_ref, xb, idb, hb, brp, gain, tri, oh, pt, probs, prb, pstage,
                    lsem, psem, ssem, rsem, isend, irecv, gsend, grecv):
    tok, d_model = x_hbm.shape
    experts = wr_ref.shape[0]
    half = tok // 2
    me = lax.axis_index('ep')
    load_x = pltpu.make_async_copy(x_hbm, xb.at[0], lsem.at[0])
    load_ids = pltpu.make_async_copy(ids_hbm, idb.at[0], lsem.at[1])
    load_x.start()
    load_ids.start()
    small = [pltpu.make_async_copy(a, b, lsem.at[k + 2]) for k, (a, b) in enumerate([(g_hbm, g_ref), (wr_hbm, wr_ref), (br_hbm, br_ref)])]
    for c in small:
        c.start()
    barrier = pltpu.get_barrier_semaphore()
    for r in range(1, 8):
        pl.semaphore_signal(barrier, inc=1, device_id={'ep': flip(me, r)}, device_id_type=MESH)
    load_x.wait()
    load_ids.wait()
    pl.semaphore_wait(barrier, 7)

    def piece(src_role, h, dst_role, to_role, k):
        rows = pl.ds(h * half, half)
        return remote(xb.at[src_role, rows], xb.at[dst_role, rows], ssem.at[k], rsem.at[dst_role, h], flip(me, to_role))

    def landed(role, h):
        piece(role, h, role, 1, 0).wait_recv()

    sends = [(0, 0, 2, 2), (0, 1, 4, 4), (0, 0, 1, 1), (0, 1, 1, 1), (0, 1, 2, 2), (0, 0, 4, 4)]
    relays = [(2, 0, 6, 4), (2, 0, 3, 1), (4, 1, 6, 2), (4, 1, 5, 1), (2, 1, 3, 1), (4, 0, 5, 1)]
    last = [(6, 0, 7, 1), (6, 1, 7, 1)]
    everything = sends + relays + last

    def go(k):
        piece(*everything[k], k).start()

    for k in range(6):
        go(k)
    ids_out = [remote(idb.at[0], idb.at[r], isend.at[r], irecv.at[r], flip(me, r)) for r in range(1, 8)]
    for c in ids_out:
        c.start()

    for c in small:
        c.wait()
    brp[...] = jnp.zeros_like(brp)
    brp[0:1, :experts] = br_ref[...].astype(F32)
    bias = jnp.transpose(jnp.broadcast_to(brp[0:1, :], (tok, tok)))[:experts]
    gain[...] = g_ref[...].astype(F32).reshape(gain.shape)
    tri[...] = (lax.broadcasted_iota(jnp.int32, (tok, tok), 0) < lax.broadcasted_iota(jnp.int32, (tok, tok), 1)).astype(F32).astype(BF16)
    cnt_ref[...] = jnp.zeros_like(cnt_ref)

    def normed(i):
        def norm(j, c):
            rows = pl.ds(pl.multiple_of(j * 32, 32), 32)
            xf = xb[i, rows, :].astype(F32)
            inv = lax.rsqrt(jnp.mean(xf * xf, axis=-1, keepdims=True) + EPSILON)
            hb[rows, :] = (xf * inv * gain[...]).astype(BF16)
            return c

        lax.fori_loop(0, tok // 32, norm, 0)

    normed(0)
    logits = lax.dot_general(wr_ref[...], hb[...], (((1,), (1,)), ((), ())), preferred_element_type=F32) + bias
    expert_no = lax.broadcasted_iota(jnp.int32, (experts, tok), 0)
    chosen = jnp.zeros((experts, tok), F32)
    for k in range(top_k):
        chosen = jnp.where(expert_no == idb[0, k:k + 1, :], 1.0, chosen)
    picked = jnp.where(chosen > 0, logits, -jnp.inf)
    ex = jnp.exp(picked - jnp.max(picked, axis=0, keepdims=True))
    probs[...] = ex / jnp.sum(ex, axis=0, keepdims=True)

    def block(device):
        return probs.at[pl.ds(pl.multiple_of(device * local_exp, local_exp), local_exp)]

    gates_out = [remote(block(flip(me, r)), prb.at[r], gsend.at[r], grecv.at[r], flip(me, r)) for r in range(1, 8)]
    for c in gates_out:
        c.start()
    prb[0] = probs[pl.ds(pl.multiple_of(me * local_exp, local_exp), local_exp), :]

    def plan(i, carry):
        @pl.when(i >= 1)
        def _():
            remote(idb.at[i], idb.at[i], isend.at[0], irecv.at[i], flip(me, 1)).wait_recv()
            remote(prb.at[i], prb.at[i], gsend.at[0], grecv.at[i], flip(me, 1)).wait_recv()

        src = flip(me, i)
        slot = lax.rem(i, 2)
        out_p = pltpu.make_async_copy(pstage.at[slot], pm_hbm.at[src], psem.at[slot])
        ids = idb[i]
        number = me * local_exp + lax.broadcasted_iota(jnp.int32, (local_exp, tok), 0)
        held = jnp.zeros((local_exp, tok), F32)
        for k in range(top_k):
            held = jnp.where(number == ids[k:k + 1, :], 1.0, held)
        rank = jnp.dot(held.astype(BF16), tri[...], preferred_element_type=F32)
        count = jnp.sum(held, axis=1, keepdims=True)
        lane = lax.broadcasted_iota(jnp.int32, cnt_ref.shape, 1)
        cnt_ref[...] = jnp.where(lane == src, count.astype(jnp.int32), cnt_ref[...])
        rank = jnp.where(held > 0, rank, -1.0)
        place = lax.broadcasted_iota(jnp.int32, (cap, tok), 0).astype(F32)
        p_loc = prb[i]
        for e in range(local_exp):
            hit = rank[e:e + 1, :] == place
            oh[i, e * cap:(e + 1) * cap, :] = jnp.where(hit, 1.0, 0.0).astype(BF16)
            pt[e * cap:(e + 1) * cap, :] = jnp.where(hit, p_loc[e:e + 1, :], 0.0)

        @pl.when(i >= 2)
        def _():
            out_p.wait()

        for b in range(local_exp * cap // tok):
            p = jnp.transpose(pt[b * tok:(b + 1) * tok, :])
            for part in range(3):
                low = p.astype(BF16)
                pstage[slot, part * tok:(part + 1) * tok, b * tok:(b + 1) * tok] = low
                p = p - low.astype(F32)
        out_p.start()
        return carry

    lax.fori_loop(0, 8, plan, 0)
    save_cnt = pltpu.make_async_copy(cnt_ref, cnt_hbm, lsem.at[0])
    save_cnt.start()

    def gather(i, carry):
        @pl.when(i == 1)
        def _():
            landed(1, 0)
            landed(1, 1)

        @pl.when(i == 2)
        def _():
            landed(2, 0)
            go(6)
            go(7)
            landed(4, 1)
            go(8)
            go(9)
            landed(2, 1)
            go(10)
            landed(4, 0)
            go(11)

        @pl.when(i == 3)
        def _():
            landed(3, 0)
            landed(3, 1)

        @pl.when(i == 5)
        def _():
            landed(5, 0)
            landed(5, 1)

        @pl.when(i == 6)
        def _():
            landed(6, 0)
            go(12)
            landed(6, 1)
            go(13)

        @pl.when(i == 7)
        def _():
            landed(7, 0)
            landed(7, 1)

        normed(i)
        src = flip(me, i)
        for n in range(0, d_model, 512):
            rows = jnp.dot(oh[i], hb[:, n:n + 512], preferred_element_type=F32).astype(BF16)
            for e in range(local_exp):
                xs_ref[e, src, :, n:n + 512] = rows[e * cap:(e + 1) * cap, :]
        return carry

    lax.fori_loop(0, 8, gather, 0)
    save_cnt.wait()
    for slot in range(2):
        pltpu.make_async_copy(pstage.at[slot], pm_hbm.at[me], psem.at[slot]).wait()
    for c in ids_out + gates_out:
        c.wait_send()
    for k in range(len(everything)):
        piece(*everything[k], k).wait_send()


def gate_up_kernel(cnt_hbm, xs_ref, wgu_hbm, bgu_hbm, z_ref, wb, xc, zc, uc, braw, bias, perm, cnt, blk, total, wsem, sem):
    local_exp, n_src, cap, d_model = xs_ref.shape
    width = wgu_hbm.shape[2]
    per_src = cap // BLK
    n_slot = wb.shape[0]

    def load_w(e):
        slot = lax.rem(e, n_slot)
        return pltpu.make_async_copy(wgu_hbm.at[e], wb.at[slot], wsem.at[slot])

    load_cnt = pltpu.make_async_copy(cnt_hbm, cnt, sem.at[0])
    load_bias = pltpu.make_async_copy(bgu_hbm, braw, sem.at[1])
    load_cnt.start()
    load_bias.start()
    for e in range(n_slot):
        load_w(e).start()
    row = lax.broadcasted_iota(jnp.int32, perm.shape, 0)
    col = lax.broadcasted_iota(jnp.int32, perm.shape, 1)
    source = jnp.where(col < 128, 2 * col, 2 * col - 255)
    perm[...] = jnp.where(row == source, 1.0, 0.0).astype(BF16)
    load_cnt.wait()

    def listed(e, carry):
        z_ref[e] = jnp.zeros(z_ref.shape[1:], BF16)
        n = jnp.int32(0)
        prev = jnp.int32(0)
        for s in range(n_src):
            k = lax.div(cnt[e, s] + (BLK - 1), BLK)
            for b in range(per_src):
                prev = jnp.where(b < k, s * per_src + b, prev)
                blk[e, n + b] = prev
            n = n + k
        for j in range(n_src * per_src):
            @pl.when(j >= n)
            def _():
                blk[e, j] = prev
        total[e] = n
        return carry

    lax.fori_loop(0, local_exp, listed, 0)
    load_bias.wait()
    bias[...] = braw[...].astype(F32)

    def expert(e, carry):
        slot = lax.rem(e, n_slot)
        load_w(e).wait()

        def run(rows):
            n = rows // BLK
            for j in range(n):
                b = blk[e, j]
                first = pl.multiple_of(lax.rem(b, per_src) * BLK, BLK)
                xc[j * BLK:(j + 1) * BLK, :] = xs_ref[e, lax.div(b, per_src), pl.ds(first, BLK), :]
            for n0 in range(0, width, NSTEP):
                w = min(NSTEP, width - n0)
                u = jnp.dot(xc[0:rows, :], wb[slot, :, n0:n0 + w], preferred_element_type=F32) + bias[pl.ds(e, 1), n0:n0 + w]
                uc[0:rows, n0:n0 + w] = jnp.minimum(jnp.maximum(u, LOWEST), LIMIT).astype(BF16)
            for m in range(0, width, 256):
                v = jnp.dot(uc[0:rows, m:m + 256], perm[...], preferred_element_type=F32)
                gate = v[:, :128]
                linear = jnp.maximum(v[:, 128:], -LIMIT)
                z = gate * lax.logistic(ALPHA * gate) * (linear + 1.0)
                zc[0:rows, m // 2:m // 2 + 128] = z.astype(BF16)
            for j in range(n):
                z_ref[e, pl.ds(pl.multiple_of(blk[e, j] * BLK, BLK), BLK), :] = zc[j * BLK:(j + 1) * BLK, :]

        n = total[e]

        @pl.when(jnp.logical_and(n > 0, n <= 8))
        def _():
            run(128)

        @pl.when(jnp.logical_and(n > 8, n <= 16))
        def _():
            run(256)

        @pl.when(n > 16)
        def _():
            run(384)

        @pl.when(e + n_slot < local_exp)
        def _():
            load_w(e + n_slot).start()
        return carry

    lax.fori_loop(0, local_exp, expert, 0)


def combine_kernel(z_ref, pm_hbm, wd_hbm, bd_hbm, x_hbm, out_ref,
                   bd_ref, x_ref, pm, wb, bias, yb, part, in0, in1, in2,
                   psem, lsem, wsem, s0, s1, s2, r0, r1, r2):
    local_exp, rows_all, d_ff = z_ref.shape
    n_src = 8
    cap = rows_all // n_src
    tok, d_model = x_hbm.shape
    n_col = d_model // COLS
    half = COLS // 2
    me = lax.axis_index('ep')
    barrier = pltpu.get_barrier_semaphore()
    for r in (1, 2, 4):
        pl.semaphore_signal(barrier, inc=1, device_id={'ep': flip(me, r)}, device_id_type=MESH)

    def load_w(c):
        slot = lax.rem(c, 2)
        cols = pl.ds(pl.multiple_of(c * COLS, COLS), COLS)
        return pltpu.make_async_copy(wd_hbm.at[:, :, cols], wb.at[slot], wsem.at[slot])

    load_w(0).start()
    pload = pltpu.make_async_copy(pm_hbm, pm, psem)
    pload.start()
    bload = pltpu.make_async_copy(bd_hbm, bd_ref, lsem.at[0])
    xload = pltpu.make_async_copy(x_hbm, x_ref, lsem.at[1])
    bload.start()
    xload.start()
    bload.wait()
    bias[...] = bd_ref[...].astype(F32)

    def to_mate(c):
        return remote(part.at[c, 1], in0.at[c], s0.at[c], r0.at[c], flip(me, 1))

    def to_first(c, h):
        return remote(part.at[c, 0, h, pl.ds(2, 2)], in1.at[c, h], s1.at[c, h], r1.at[c, h], flip(me, 2 + 2 * h))

    def to_second(c, h):
        return remote(part.at[c, 0, h, 1], in2.at[c, h], s2.at[c, h], r2.at[c, h], flip(me, 4 - 2 * h))

    def merge_mate(c):
        to_mate(c).wait_recv()
        for js in ((2, 3), (0, 1)):
            for h in range(2):
                for j in js:
                    part[c, 0, h, j] = part[c, 0, h, j] + in0[c, h, j]
                if js[0] == 2:
                    to_first(c, h).start()

    def merge_first(c):
        for h in range(2):
            to_first(c, h).wait_recv()
            for j in (1, 0):
                part[c, 0, h, j] = part[c, 0, h, j] + in1[c, h, j]
            to_second(c, h).start()

    def finish(c):
        for h in range(2):
            to_second(c, h).wait_recv()
            cols = pl.ds(pl.multiple_of(c * COLS + h * half, half), half)
            out_ref[:, cols] = (x_ref[:, cols].astype(F32) + (part[c, 0, h, 0] + in2[c, h])).astype(BF16)

    def step(c, carry):
        slot = lax.rem(c, 2)
        cols = pl.ds(pl.multiple_of(c * COLS, COLS), COLS)

        @pl.when(c + 1 < n_col)
        def _():
            load_w(c + 1).start()

        load_w(c).wait()
        for e in range(local_exp):
            y = jnp.dot(z_ref[e], wb[slot, e], preferred_element_type=F32) + bias[e:e + 1, cols]
            y = y.astype(BF16)
            for s in range(n_src):
                yb[s, e * cap:(e + 1) * cap, :] = y[s * cap:(s + 1) * cap, :]

        @pl.when(c == 0)
        def _():
            pload.wait()
            xload.wait()
            pl.semaphore_wait(barrier, 3)

        @pl.when(c >= 1)
        def _():
            merge_mate(c - 1)

        for core in (1, 0):
            for q in range(4):
                src = flip(me, 2 * q + core)
                sums = jnp.dot(pm[src], yb[src], preferred_element_type=F32)
                sums = (sums[2 * tok:] + sums[tok:2 * tok]) + sums[:tok]
                for h in range(2):
                    j = q if h == 1 or q in (0, 3) else 3 - q
                    part[c, core, h, j] = sums[:, h * half:(h + 1) * half]

        to_mate(c).start()

        @pl.when(c >= 2)
        def _():
            merge_first(c - 2)

        @pl.when(c >= 4)
        def _():
            finish(c - 4)
        return carry

    lax.fori_loop(0, n_col, step, 0)
    merge_mate(n_col - 1)
    for c in range(n_col - 2, n_col):
        merge_first(c)
    for c in range(n_col - 4, n_col):
        finish(c)
    for c in range(n_col):
        to_mate(c).wait_send()
        for h in range(2):
            to_first(c, h).wait_send()
            to_second(c, h).wait_send()


def solution(mesh):
    n_group = mesh.shape['ep']
    assert n_group == 8
    rows_spec = P(('dp', 'ep'), None)

    def local_block(x_in, expert_ids, norm_weight, router_w, router_b, w_gate_up, b_gate_up, w_down, b_down):
        tok, d_model = x_in.shape
        top_k = expert_ids.shape[1]
        local_exp, _, width = w_gate_up.shape
        d_ff = w_down.shape[1]
        experts = local_exp * n_group
        cap = CAPACITY_FACTOR * top_k * tok // experts
        rows_all = n_group * cap
        hbm = pl.BlockSpec(memory_space=pl.ANY)
        vmem = pl.BlockSpec(memory_space=pltpu.VMEM)
        smem = pl.BlockSpec(memory_space=pltpu.SMEM)
        dma = pltpu.SemaphoreType.DMA
        in_hbm = functools.partial(pltpu.with_memory_space_constraint, memory_space=pltpu.HBM)
        pinned = functools.partial(pltpu.with_memory_space_constraint, memory_space=pltpu.VMEM)
        xs, pm, counts = pl.pallas_call(
            functools.partial(dispatch_kernel, top_k, local_exp, cap),
            out_shape=(pltpu.VMEM((local_exp, n_group, cap, d_model), BF16),
                       pltpu.HBM((n_group, 3 * tok, local_exp * cap), BF16),
                       pltpu.HBM((local_exp, 128), jnp.int32)),
            in_specs=[hbm] * 5,
            out_specs=(vmem, hbm, hbm),
            scratch_shapes=[
                pltpu.VMEM((d_model,), BF16), pltpu.VMEM((experts, d_model), BF16), pltpu.VMEM((1, experts), BF16), pltpu.VMEM((local_exp, 128), jnp.int32),
                pltpu.VMEM((8, tok, d_model), BF16), pltpu.VMEM((8, top_k, tok), jnp.int32), pltpu.VMEM((tok, d_model), BF16),
                pltpu.VMEM((8, 128), F32), pltpu.VMEM((1, d_model), F32), pltpu.VMEM((tok, tok), BF16),
                pltpu.VMEM((8, local_exp * cap, tok), BF16), pltpu.VMEM((local_exp * cap, tok), F32),
                pltpu.VMEM((experts, tok), F32), pltpu.VMEM((8, local_exp, tok), F32),
                pltpu.VMEM((2, 3 * tok, local_exp * cap), BF16),
                dma((5,)), dma((2,)), dma((14,)), dma((8, 2)), dma((8,)), dma((8,)), dma((8,)), dma((8,))],
            compiler_params=pltpu.CompilerParams(collective_id=0, has_side_effects=True, vmem_limit_bytes=11 * MIB),
            name='dispatch',
        )(*map(in_hbm, (x_in, expert_ids.T, norm_weight, router_w.T, router_b.reshape(1, experts))))
        z = pl.pallas_call(
            gate_up_kernel,
            out_shape=pltpu.VMEM((local_exp, rows_all, d_ff), BF16),
            in_specs=[hbm, vmem, hbm, hbm],
            out_specs=vmem,
            scratch_shapes=[
                pltpu.VMEM((N_RING, d_model, width), BF16),
                pltpu.VMEM((rows_all, d_model), BF16), pltpu.VMEM((rows_all, d_ff), BF16), pltpu.VMEM((rows_all, width), BF16),
                pltpu.VMEM((local_exp, width), BF16), pltpu.VMEM((local_exp, width), F32), pltpu.VMEM((256, 256), BF16),
                pltpu.SMEM((local_exp, 128), jnp.int32), pltpu.SMEM((local_exp, 2 * rows_all // BLK), jnp.int32), pltpu.SMEM((local_exp,), jnp.int32),
                dma((N_RING,)), dma((2,))],
            compiler_params=pltpu.CompilerParams(vmem_limit_bytes=42 * MIB),
            name='gate_up',
        )(counts, pinned(xs), w_gate_up, in_hbm(b_gate_up))
        n_col = d_model // COLS
        return pl.pallas_call(
            combine_kernel,
            out_shape=pltpu.VMEM((tok, d_model), BF16),
            in_specs=[vmem, hbm, hbm, hbm, hbm],
            out_specs=vmem,
            scratch_shapes=[
                pltpu.VMEM((local_exp, d_model), BF16), pltpu.VMEM((tok, d_model), BF16),
                pltpu.VMEM((n_group, 3 * tok, local_exp * cap), BF16),
                pltpu.VMEM((2, local_exp, d_ff, COLS), BF16), pltpu.VMEM((local_exp, d_model), F32),
                pltpu.VMEM((n_group, local_exp * cap, COLS), BF16), pltpu.VMEM((n_col, 2, 2, 4, tok, COLS // 2), F32),
                pltpu.VMEM((n_col, 2, 4, tok, COLS // 2), F32), pltpu.VMEM((n_col, 2, 2, tok, COLS // 2), F32),
                pltpu.VMEM((n_col, 2, tok, COLS // 2), F32),
                dma, dma((2,)), dma((2,)), dma((n_col,)), dma((n_col, 2)), dma((n_col, 2)), dma((n_col,)), dma((n_col, 2)), dma((n_col, 2))],
            compiler_params=pltpu.CompilerParams(collective_id=1, has_side_effects=True, vmem_limit_bytes=40 * MIB),
            name='combine',
        )(pinned(z), in_hbm(pm), w_down, in_hbm(b_down), in_hbm(x_in))

    return jax.shard_map(local_block, mesh=mesh, in_specs=(rows_spec, rows_spec, P(), P(), P(), P('ep', None, None), P('ep', None), P('ep', None, None), P('ep', None)), out_specs=rows_spec, check_vma=False)
```

time: 142 us -> 114 us (0.80)
  Pallas kernels: 136 us -> 113 us
  local copies, waits for them, and re-layouts: 6.4 us -> 0.8 us
    pallas_call x2, Pallas kernels: 103 us -> 80.3 us  [the longest x1 50.7 us: local_block(): pl.pallas_call(combine_kernel, out_shape=pltpu.VMEM((tok, d_model), BF16)...]
    unnamed x2 -> x1, local copies, waits for them, and re-layouts: 3.83 us -> 0.8 us
where the time goes in v2:
time: 114 us
  Pallas kernels  113 us (99%)
    pallas_call x1, Pallas kernels, local_block(): pl.pallas_call(combine_kernel, out_shape=pltpu.VMEM((tok, d_model), BF16)...  50.7 us
    pallas_call x1, Pallas kernels, local_block(): pl.pallas_call(functools.partial(dispatch_kernel, top_k, local_exp, cap),...  32.8 us
    pallas_call x1, Pallas kernels, local_block(): pl.pallas_call(gate_up_kernel, out_shape=pltpu.VMEM((local_exp, rows_all,...  29.5 us

profile of v2, /device:TPU:0, one launch (start us, length us, event | category | flops | bytes accessed | tf_op | source)
XLA Modules:
  0.0 113.9 jit_solution(5179485148143228063)
XLA Ops:
  0.0 32.8 %dispatch.1 = (bf16[8,8,48,2048]{3,2,1,0:T(8,128)(2,1)S(1)}, bf16[8,384,384]{2,1,0:T(8,128)(2,1)}, s32[8,128]{1,0:T(8,128)}) custom-call(bf16[128,2048]{1,0:T(8,128)(2,1)} %x_hbm.3, s32[6,128]{1,0:T(8,128)} %bitcast.4, bf16[2048]{0:T(1024)(128)(2,1)} %g_hbm.1, bf16[64,2048]{1,0:T(8,128)(2,1)} %bitcast.3, bf16[1,64]{1,0:T(2,128)(2,1)} %bitcast.5), custom_call_target="tpu_custom_call" | custom-call | tf_op jit(solution)/shard_map/dispatch/pallas_call | solution.py:442
  32.8 29.5 %gate_up.1.z_ref = bf16[8,384,1408]{2,1,0:T(8,128)(2,1)S(1)} custom-call(s32[8,128]{1,0:T(8,128)} %get-tuple-element.8.cnt_hbm, bf16[8,8,48,2048]{3,2,1,0:T(8,128)(2,1)S(1)} %get-tuple-element.9.xs_ref, bf16[8,2048,2816]{2,1,0:T(8,128)(2,1)} %wgu_hbm.1, bf16[8,2816]{1,0:T(8,128)(2,1)} %bgu_hbm.1), custom_call_target="tpu_custom_call" | custom-call | tf_op jit(solution)/shard_map/gate_up/pallas_call | solution.py:460
  62.3 50.7 %combine.1 = bf16[128,2048]{1,0:T(8,128)(2,1)S(1)} custom-call(bf16[8,384,1408]{2,1,0:T(8,128)(2,1)S(1)} %gate_up.1.z_ref, bf16[8,384,384]{2,1,0:T(8,128)(2,1)} %get-tuple-element.10.pm_hbm, bf16[8,1408,2048]{2,1,0:T(8,128)(2,1)} %wd_hbm.1, bf16[8,2048]{1,0:T(8,128)(2,1)} %bd_hbm.1, bf16[128,2048]{1,0:T(8,128)(2,1)} %x_hbm.3), custom_call_target="tpu_custom_call" | custom-call | tf_op jit(solution)/shard_map/combine/pallas_call | solution.py:475
  113.1 0.8 copy.11
